TPU v7x, 32 devices: a whole 2x2x4 slice. The times are simulated.
32 devices in a mesh: grp: 16 (over z, y, x), sub: 2 (over core).
Axes of the slice: x: 2, y: 2, z: 4, core: 2. Of those that a mesh axis runs over, the one named last changes fastest.
Arguments:
- potentials: bfloat16 [1024, 200, 200], P(('grp', 'sub')), may hold values from -6 to 6
- dimers: int32 [4096, 2], P(('grp', 'sub')), may hold values from 0 to 1023, as said below
- coupling: float32 [4096], P(('grp', 'sub')), may hold values from 0.3 to 1.5
- transform: bfloat16 [400, 400], replicated, may hold values from -0.3125 to 0.3125
Outputs:
- energies: float32 [4096, 400], P(('grp', 'sub'))
- checksum: float32 [1], replicated
Inputs may be any that keep to these rules, and one draw needn't show every extreme that they name: `dimers`: each row names two different fragments. Rows d with d // 128 = o belong to owner o, and their second fragment f has f // 32 = o. Among the 128 first fragments of one owner's rows, at most 6 fall into the fragments of any one device (fragments f with f // 32 equal), and exactly 6 into some device's fragments.
All inputs are finite; a program needn't handle non-finite values.
Results may differ from a plain program's by a relative error of at most 0.0023.
Values may be sent and summed in bfloat16 or wider, within the bound.
No kernel may reach another device: no remote copies, remote signals or barrier semaphores. Data moves between devices by JAX's collectives and lax.ppermute only.
A program may use at most 192 MiB of HBM per device.

v0:
```python
import jax
import jax.numpy as jnp
from jax import lax
from jax.sharding import PartitionSpec as P


def block_energies(left, right, scale, transform, basis):
    upper = transform[:basis]
    lower = transform[basis:]
    cross = jnp.einsum("nab,nbc->nac", left, right, preferred_element_type=jnp.float32)
    block = (cross * (scale[:, None, None] / jnp.sqrt(jnp.float32(basis)))).astype(jnp.bfloat16)
    top = jnp.einsum("nab,bk->nak", left, upper, preferred_element_type=jnp.float32)
    top = top + jnp.einsum("nab,bk->nak", block, lower, preferred_element_type=jnp.float32)
    bottom = jnp.einsum("nab,ak->nbk", block, upper, preferred_element_type=jnp.float32)
    bottom = bottom + jnp.einsum("nab,bk->nak", right, lower, preferred_element_type=jnp.float32)
    upper_f = upper.astype(jnp.float32)
    lower_f = lower.astype(jnp.float32)
    return jnp.sum(upper_f[None] * top, axis=1) + jnp.sum(lower_f[None] * bottom, axis=1)


def local(potentials, dimers, coupling, transform):
    frag_dev, basis, _ = potentials.shape
    count = dimers.shape[0]
    owners = lax.axis_size(("grp", "sub"))
    cap = max(2, (4 * count + 3 * owners - 1) // (3 * owners))
    wanted = dimers[:, 0]
    source = wanted // frag_dev
    onehot = (source[:, None] == jnp.arange(owners, dtype=jnp.int32)[None, :]).astype(jnp.int32)
    ranking = jnp.sum(jnp.cumsum(onehot, axis=0) * onehot, axis=1) - 1
    slots = source * cap + ranking
    requests = jnp.zeros((owners * cap,), jnp.int32).at[slots].set(wanted % frag_dev)
    asked = lax.all_to_all(
        requests.reshape(owners, cap), ("grp", "sub"), split_axis=0, concat_axis=0, tiled=True
    )
    served = jnp.take(potentials, asked.reshape(-1), axis=0).reshape(owners, cap, basis, basis)
    arrived = lax.all_to_all(served, ("grp", "sub"), split_axis=0, concat_axis=0, tiled=True)
    leading = jnp.take(arrived.reshape(owners * cap, basis, basis), slots, axis=0)
    trailing = jnp.take(potentials, dimers[:, 1] % frag_dev, axis=0)
    width = 8
    leading = leading.reshape(count // width, width, basis, basis)
    trailing = trailing.reshape(count // width, width, basis, basis)
    scales = coupling.reshape(count // width, width)

    def one_block(item):
        left, right, scale = item
        return block_energies(left, right, scale, transform, basis)

    energies = lax.map(one_block, (leading, trailing, scales)).reshape(count, 2 * basis)
    total = count * owners
    position = lax.axis_index(("grp", "sub")) * count + jnp.arange(count, dtype=jnp.int32)
    weights = (position.astype(jnp.float32) + 1.0) / total
    partial_value = 2.0 / total * jnp.sum(weights * jnp.mean(energies * energies, axis=1))
    checksum = lax.psum(partial_value, ("grp", "sub"))
    return (energies, checksum.reshape(1))


def solution(mesh):
    in_specs = (P(("grp", "sub"), None, None), P(("grp", "sub"), None), P(("grp", "sub")), P())
    out_specs = (P(("grp", "sub"), None), P())
    return jax.shard_map(local, mesh=mesh, in_specs=in_specs, out_specs=out_specs, check_vma=False)
```

profile of v0, /device:TPU:12, one launch (start us, length us, event | category | flops | bytes accessed | tf_op | source)
XLA Modules:
  0.0 666.5 jit_solution(18246285668778304363)
XLA Ops:
  0.6 0.8 fusion.30
  1.5 0.8 and_select_fusion.1
  2.8 1.3 and_reduce_fusion
  4.0 1.0 scatter_custom_fusion
  5.1 10.9 %all_to_all.14 = s32[32,1,6]{2,1,0:T(1,128)S(1)} all-to-all(s32[32,1,6]{2,1,0:T(1,128)S(1)} %bitcast.75), channel_id=1, replica_groups=mesh['grp'=16,'sub'=2] {'grp','sub'}, dimensions={0} | all-to-all | bytes 1536 | tf_op jit(solution)/shard_map/all_to_all | solution.py:32
  17.5 10.6 %gather_fusion = bf16[192,200,200]{2,1,0:T(8,128)(2,1)} fusion(bf16[32,200,200]{2,1,0:T(8,128)(2,1)S(1)} %copy-done, s32[1024]{0:T(1024)S(1)} %pad_clamp_fusion.2), kind=kCustom, calls=%fused_computation | custom fusion | bytes 30720768 | tf_op jit(solution)/shard_map/jit(_take)/gather | solution.py:35
  28.1 17.0 %broadcast_select_fusion = bf16[32,6,200,200]{3,2,1,0:T(8,128)(2,1)} fusion(bf16[32,6,200,200]{3,2,1,0:T(8,128)(2,1)} %bitcast.70, pred[32,6]{1,0:T(8,128)(4,1)S(1)} %compare_and_fusion), kind=kLoop, calls=%fused_computation.34 | loop fusion | flops 7680000 | bytes 30720192 | tf_op jit(solution)/shard_map/jit(_take)/select_n | solution.py:35
  45.1 5.9 all-to-all-start.1
  51.8 8.7 %gather_fusion.2 = bf16[128,200,200]{2,1,0:T(8,128)(2,1)} fusion(bf16[32,200,200]{2,1,0:T(8,128)(2,1)S(1)} %copy-done, s32[1024]{0:T(1024)S(1)} %pad_clamp_fusion), kind=kCustom, calls=%fused_computation.2 | custom fusion | bytes 20480512 | tf_op jit(solution)/shard_map/jit(_take)/gather | solution.py:38
  61.3 10.1 %broadcast_select_fusion.1 = bf16[16,8,200,200]{3,2,1,0:T(8,128)(2,1)} fusion(bf16[16,8,200,200]{3,2,1,0:T(8,128)(2,1)} %bitcast.71, pred[16,8]{1,0:T(8,128)(4,1)S(1)} %broadcast_in_dim.59), kind=kLoop, calls=%fused_computation.35 | loop fusion | flops 5120000 | bytes 20480128 | tf_op jit(solution)/shard_map/jit(_take)/select_n | solution.py:38
  71.5 401.6 %all-to-all-done.1 = bf16[32,6,200,200]{3,2,1,0:T(8,128)(2,1)} async-done(((bf16[32,6,200,200]{3,2,1,0:T(8,128)(2,1)}), bf16[32,6,200,200]{3,2,1,0:T(8,128)(2,1)}, u32[]{:S(2)}, u32[]{:S(2)}) %all-to-all-start.1) | async-done | bytes 15360032 | tf_op jit(solution)/shard_map/all_to_all | solution.py:36
  473.1 15.3 %gather_fusion.1 = bf16[128,200,200]{2,1,0:T(8,128)(2,1)} fusion(bf16[192,200,200]{2,1,0:T(8,128)(2,1)} %bitcast.14, s32[1024]{0:T(1024)S(1)} %pad_clamp_fusion.1), kind=kCustom, calls=%fused_computation.1 | custom fusion | bytes 20480512 | tf_op jit(solution)/shard_map/jit(_take)/gather | solution.py:37
  488.3 10.2 %broadcast_select_fusion.2 = bf16[16,8,200,200]{3,2,1,0:T(8,128)(2,1)} fusion(bf16[16,8,200,200]{3,2,1,0:T(8,128)(2,1)} %bitcast.72, pred[16,8]{1,0:T(8,128)(4,1)S(1)} %broadcast_in_dim.51), kind=kLoop, calls=%fused_computation.36 | loop fusion | flops 5120000 | bytes 20480128 | tf_op jit(solution)/shard_map/jit(_take)/select_n | solution.py:37
  498.6 110.3 %while.10 = (s32[]{:T(128)}, f32[16,8,400]{2,1,0:T(8,128)S(1)}, bf16[400,400]{1,0:T(8,128)(2,1)S(1)}, bf16[16,8,200,200]{3,2,1,0:T(8,128)(2,1)}, bf16[16,8,200,2...) while((s32[]{:T(128)}, f32[16,8,400]{2,1,0:T(8,128)S(1)}, bf16[400,400]{1,0:T(8,128)(2,1)S(1)}, ...), condition=%wide.region_6.7_spmd, body=%wide.region_3.6_spmd.sunk | while | flops 1156636800 | bytes 19904180 | solution.py:48
  498.6 1.8 multiply_convert_fusion.2
  500.3 1.7 fusion.54
  503.6 1.9 multiply_reduce_fusion.7
  505.5 1.8 multiply_convert_fusion.2
  507.2 1.7 fusion.54
  510.5 1.9 multiply_reduce_fusion.7
  512.4 1.8 multiply_convert_fusion.2
  514.1 1.7 fusion.54
  517.3 1.9 multiply_reduce_fusion.7
  519.3 1.8 multiply_convert_fusion.2
  521.0 1.7 fusion.54
  524.2 1.9 multiply_reduce_fusion.7
  526.2 1.8 multiply_convert_fusion.2
  527.9 1.7 fusion.54
  531.1 1.9 multiply_reduce_fusion.7
  533.1 1.8 multiply_convert_fusion.2
  534.8 1.7 fusion.54
  538.0 1.9 multiply_reduce_fusion.7
  539.9 1.8 multiply_convert_fusion.2
  541.7 1.7 fusion.54
  544.9 1.9 multiply_reduce_fusion.7
  546.8 1.8 multiply_convert_fusion.2
  548.6 1.7 fusion.54
  551.8 1.9 multiply_reduce_fusion.7
  553.7 1.8 multiply_convert_fusion.2
  555.5 1.7 fusion.54
  558.7 1.9 multiply_reduce_fusion.7
  560.6 1.8 multiply_convert_fusion.2
  562.4 1.7 fusion.54
  565.6 1.9 multiply_reduce_fusion.7
  567.5 1.8 multiply_convert_fusion.2
  569.3 1.7 fusion.54
  572.5 1.9 multiply_reduce_fusion.7
  574.4 1.8 multiply_convert_fusion.2
  576.2 1.7 fusion.54
  579.4 1.9 multiply_reduce_fusion.7
  581.3 1.8 multiply_convert_fusion.2
  583.1 1.7 fusion.54
  586.3 1.9 multiply_reduce_fusion.7
  588.2 1.8 multiply_convert_fusion.2
  590.0 1.7 fusion.54
  593.2 1.9 multiply_reduce_fusion.7
  595.1 1.8 multiply_convert_fusion.2
  596.9 1.7 fusion.54
  600.1 1.9 multiply_reduce_fusion.7
  602.0 1.8 multiply_convert_fusion.2
  603.8 1.7 fusion.54
  607.0 1.9 multiply_reduce_fusion.7
  610.5 55.1 %psum.7 = f32[1]{0:T(128)} all-reduce(f32[1]{0:T(128)} %bitcast.19), channel_id=1, replica_groups=mesh['grp'=16,'sub'=2] {'grp','sub'}, use_global_device_ids=true, to_apply=%region_9.10 | all-reduce | flops 1 | bytes 8 | tf_op jit(solution)/shard_map/psum | solution.py:53
  665.6 0.8 copy.23
  (105 shorter events, 28.0 us)
Async XLA Ops:
  0.6 16.8 %copy-start = (bf16[32,200,200]{2,1,0:T(8,128)(2,1)S(1)}, bf16[32,200,200]{2,1,0:T(8,128)(2,1)}, u32[]{:S(2)}) copy-start(bf16[32,200,200]{2,1,0:T(8,128)(2,1)} %param.6) | copy-start | bytes 7680004
  45.1 427.9 %all-to-all-start.1 = ((bf16[32,6,200,200]{3,2,1,0:T(8,128)(2,1)}), bf16[32,6,200,200]{3,2,1,0:T(8,128)(2,1)}, u32[]{:S(2)}, u32[]{:S(2)}) async-start(bf16[32,6,200,200]{3,2,1,0:T(8,128)(2,1)} %broadcast_select_fusion), calls=%async_computation.1 | async-start | bytes 39321600 | tf_op jit(solution)/shard_map/all_to_all | solution.py:36
  488.3 10.2 %copy-start.2 = (bf16[400,400]{1,0:T(8,128)(2,1)S(1)}, bf16[400,400]{1,0:T(8,128)(2,1)}, u32[]{:S(2)}) copy-start(bf16[400,400]{1,0:T(8,128)(2,1)} %param.9) | copy-start | bytes 960004
  608.9 57.6 %copy-start.1 = (bf16[32,200,200]{2,1,0:T(8,128)(2,1)S(1)}, bf16[32,200,200]{2,1,0:T(8,128)(2,1)}, u32[]{:S(2)}) copy-start(bf16[32,200,200]{2,1,0:T(8,128)(2,1)} %param.6) | copy-start | bytes 7680004
where the time goes:
time: 669 us; the launch traced here: 666 us
  waiting for transfers between devices  402 us (60%)
  matrix products  108 us (16%)
  blocking collectives  66 us (10%)
  other arithmetic  44.6 us (7%)
  local copies, waits for them, and re-layouts  38.2 us (6%)
    all_to_all x1, waiting for transfers between devices, local(): lax.all_to_all(served, ('grp', 'sub'), split_axis=0, concat_axis=0, tiled...  402 us
    psum x1, blocking collectives, local(): checksum = lax.psum(partial_value, ('grp', 'sub'))  55.1 us
    dot_general x16, matrix products, block_energies(): jnp.einsum('nab,bk->nak', right, lower, preferred_element_type=jnp.float32)  29.7 us
    dot_general x16, matrix products, block_energies(): jnp.einsum('nab,nbc->nac', left, right, preferred_element_type=jnp.float32)  28.3 us
    dot_general x16, matrix products, block_energies(): jnp.einsum('nab,bk->nak', left, upper, preferred_element_type=jnp.float32)  27.7 us
    select_n x2, other arithmetic, local(): jnp.take(potentials, asked.reshape(-1), axis=0)  17 us
    gather x1, local copies, waits for them, and re-layouts, local(): jnp.take(arrived.reshape(owners * cap, basis, basis), slots, axis=0)  15.3 us
  transfers between devices with their start and end apart: 1, of which 1 were waited for; matrix products, arithmetic and copies ran while one was open for 3% of the time, Pallas kernels for 0%

commit v1 on v0

--- a/solution.py
+++ b/solution.py
@@ -50,7 +50,8 @@
     position = lax.axis_index(("grp", "sub")) * count + jnp.arange(count, dtype=jnp.int32)
     weights = (position.astype(jnp.float32) + 1.0) / total
     partial_value = 2.0 / total * jnp.sum(weights * jnp.mean(energies * energies, axis=1))
-    checksum = lax.psum(partial_value, ("grp", "sub"))
+    parts = lax.all_gather(partial_value, ("grp", "sub"))
+    checksum = jnp.sum(parts, axis=0)
     return (energies, checksum.reshape(1))
 
 

time: 669 us -> 669 us (level)
    psum x1 -> x0, blocking collectives: 55.1 us -> none  [local(): checksum = lax.psum(partial_value, ('grp', 'sub'))]
    unnamed x0 -> x1, blocking collectives: none -> 54.2 us
where the time goes in v1:
time: 669 us; the launch traced here: 666 us
  waiting for transfers between devices  402 us (60%)
  matrix products  108 us (16%)
  blocking collectives  65 us (10%)
  other arithmetic  45.2 us (7%)
  local copies, waits for them, and re-layouts  38.3 us (6%)
    all_to_all x1, waiting for transfers between devices, local(): lax.all_to_all(served, ('grp', 'sub'), split_axis=0, concat_axis=0, tiled...  402 us
    unnamed x1, blocking collectives  54.2 us
    dot_general x16, matrix products, block_energies(): jnp.einsum('nab,bk->nak', right, lower, preferred_element_type=jnp.float32)  29.7 us
    dot_general x16, matrix products, block_energies(): jnp.einsum('nab,nbc->nac', left, right, preferred_element_type=jnp.float32)  28.3 us
    dot_general x16, matrix products, block_energies(): jnp.einsum('nab,bk->nak', left, upper, preferred_element_type=jnp.float32)  27.7 us
    select_n x2, other arithmetic, local(): jnp.take(potentials, asked.reshape(-1), axis=0)  17 us
    gather x1, local copies, waits for them, and re-layouts, local(): jnp.take(arrived.reshape(owners * cap, basis, basis), slots, axis=0)  15.3 us
  transfers between devices with their start and end apart: 1, of which 1 were waited for; matrix products, arithmetic and copies ran while one was open for 3% of the time, Pallas kernels for 0%

profile of v1, /device:TPU:12, one launch (start us, length us, event | category | flops | bytes accessed | tf_op | source)
XLA Modules:
  0.0 666.2 jit_solution(16908118821796944188)
XLA Ops:
  0.6 0.8 fusion.30
  1.5 0.8 and_select_fusion.1
  2.8 1.3 and_reduce_fusion
  4.0 1.0 scatter_custom_fusion
  5.1 10.9 %all_to_all.14 = s32[32,1,6]{2,1,0:T(1,128)S(1)} all-to-all(s32[32,1,6]{2,1,0:T(1,128)S(1)} %bitcast.76), channel_id=1, replica_groups=mesh['grp'=16,'sub'=2] {'grp','sub'}, dimensions={0} | all-to-all | bytes 1536 | tf_op jit(solution)/shard_map/all_to_all | solution.py:32
  17.5 10.6 %gather_fusion = bf16[192,200,200]{2,1,0:T(8,128)(2,1)} fusion(bf16[32,200,200]{2,1,0:T(8,128)(2,1)S(1)} %copy-done, s32[1024]{0:T(1024)S(1)} %pad_clamp_fusion.2), kind=kCustom, calls=%fused_computation | custom fusion | bytes 30720768 | tf_op jit(solution)/shard_map/jit(_take)/gather | solution.py:35
  28.1 17.0 %broadcast_select_fusion = bf16[32,6,200,200]{3,2,1,0:T(8,128)(2,1)} fusion(bf16[32,6,200,200]{3,2,1,0:T(8,128)(2,1)} %bitcast.71, pred[32,6]{1,0:T(8,128)(4,1)S(1)} %compare_and_fusion), kind=kLoop, calls=%fused_computation.34 | loop fusion | flops 7680000 | bytes 30720192 | tf_op jit(solution)/shard_map/jit(_take)/select_n | solution.py:35
  45.1 5.9 all-to-all-start.1
  51.8 8.7 %gather_fusion.2 = bf16[128,200,200]{2,1,0:T(8,128)(2,1)} fusion(bf16[32,200,200]{2,1,0:T(8,128)(2,1)S(1)} %copy-done, s32[1024]{0:T(1024)S(1)} %pad_clamp_fusion), kind=kCustom, calls=%fused_computation.2 | custom fusion | bytes 20480512 | tf_op jit(solution)/shard_map/jit(_take)/gather | solution.py:38
  61.3 10.1 %broadcast_select_fusion.1 = bf16[16,8,200,200]{3,2,1,0:T(8,128)(2,1)} fusion(bf16[16,8,200,200]{3,2,1,0:T(8,128)(2,1)} %bitcast.72, pred[16,8]{1,0:T(8,128)(4,1)S(1)} %broadcast_in_dim.59), kind=kLoop, calls=%fused_computation.35 | loop fusion | flops 5120000 | bytes 20480128 | tf_op jit(solution)/shard_map/jit(_take)/select_n | solution.py:38
  71.5 401.6 %all-to-all-done.1 = bf16[32,6,200,200]{3,2,1,0:T(8,128)(2,1)} async-done(((bf16[32,6,200,200]{3,2,1,0:T(8,128)(2,1)}), bf16[32,6,200,200]{3,2,1,0:T(8,128)(2,1)}, u32[]{:S(2)}, u32[]{:S(2)}) %all-to-all-start.1) | async-done | bytes 15360032 | tf_op jit(solution)/shard_map/all_to_all | solution.py:36
  473.1 15.3 %gather_fusion.1 = bf16[128,200,200]{2,1,0:T(8,128)(2,1)} fusion(bf16[192,200,200]{2,1,0:T(8,128)(2,1)} %bitcast.14, s32[1024]{0:T(1024)S(1)} %pad_clamp_fusion.1), kind=kCustom, calls=%fused_computation.1 | custom fusion | bytes 20480512 | tf_op jit(solution)/shard_map/jit(_take)/gather | solution.py:37
  488.3 10.2 %broadcast_select_fusion.2 = bf16[16,8,200,200]{3,2,1,0:T(8,128)(2,1)} fusion(bf16[16,8,200,200]{3,2,1,0:T(8,128)(2,1)} %bitcast.73, pred[16,8]{1,0:T(8,128)(4,1)S(1)} %broadcast_in_dim.51), kind=kLoop, calls=%fused_computation.36 | loop fusion | flops 5120000 | bytes 20480128 | tf_op jit(solution)/shard_map/jit(_take)/select_n | solution.py:37
  498.6 110.3 %while.10 = (s32[]{:T(128)}, f32[16,8,400]{2,1,0:T(8,128)S(1)}, bf16[400,400]{1,0:T(8,128)(2,1)S(1)}, bf16[16,8,200,200]{3,2,1,0:T(8,128)(2,1)}, bf16[16,8,200,2...) while((s32[]{:T(128)}, f32[16,8,400]{2,1,0:T(8,128)S(1)}, bf16[400,400]{1,0:T(8,128)(2,1)S(1)}, ...), condition=%wide.region_6.7_spmd, body=%wide.region_3.6_spmd.sunk | while | flops 1156636800 | bytes 19904180 | solution.py:48
  498.6 1.8 multiply_convert_fusion.2
  500.3 1.7 fusion.54
  503.6 1.9 multiply_reduce_fusion.7
  505.5 1.8 multiply_convert_fusion.2
  507.2 1.7 fusion.54
  510.5 1.9 multiply_reduce_fusion.7
  512.4 1.8 multiply_convert_fusion.2
  514.1 1.7 fusion.54
  517.3 1.9 multiply_reduce_fusion.7
  519.3 1.8 multiply_convert_fusion.2
  521.0 1.7 fusion.54
  524.2 1.9 multiply_reduce_fusion.7
  526.2 1.8 multiply_convert_fusion.2
  527.9 1.7 fusion.54
  531.1 1.9 multiply_reduce_fusion.7
  533.1 1.8 multiply_convert_fusion.2
  534.8 1.7 fusion.54
  538.0 1.9 multiply_reduce_fusion.7
  539.9 1.8 multiply_convert_fusion.2
  541.7 1.7 fusion.54
  544.9 1.9 multiply_reduce_fusion.7
  546.8 1.8 multiply_convert_fusion.2
  548.6 1.7 fusion.54
  551.8 1.9 multiply_reduce_fusion.7
  553.7 1.8 multiply_convert_fusion.2
  555.5 1.7 fusion.54
  558.7 1.9 multiply_reduce_fusion.7
  560.6 1.8 multiply_convert_fusion.2
  562.4 1.7 fusion.54
  565.6 1.9 multiply_reduce_fusion.7
  567.5 1.8 multiply_convert_fusion.2
  569.3 1.7 fusion.54
  572.5 1.9 multiply_reduce_fusion.7
  574.4 1.8 multiply_convert_fusion.2
  576.2 1.7 fusion.54
  579.4 1.9 multiply_reduce_fusion.7
  581.3 1.8 multiply_convert_fusion.2
  583.1 1.7 fusion.54
  586.3 1.9 multiply_reduce_fusion.7
  588.2 1.8 multiply_convert_fusion.2
  590.0 1.7 fusion.54
  593.2 1.9 multiply_reduce_fusion.7
  595.1 1.8 multiply_convert_fusion.2
  596.9 1.7 fusion.54
  600.1 1.9 multiply_reduce_fusion.7
  602.0 1.8 multiply_convert_fusion.2
  603.8 1.7 fusion.54
  607.0 1.9 multiply_reduce_fusion.7
  610.7 54.2 %all-reduce = f32[32]{0:T(128)S(1)} all-reduce(f32[32]{0:T(128)S(1)} %dynamic-update-slice), channel_id=1, replica_groups=mesh['grp'=16,'sub'=2] {'grp','sub'}, use_global_device_ids=true, to_apply=%add | all-reduce | flops 32 | bytes 256
  665.4 0.8 copy.23
  (108 shorter events, 28.7 us)
Async XLA Ops:
  0.6 16.8 %copy-start = (bf16[32,200,200]{2,1,0:T(8,128)(2,1)S(1)}, bf16[32,200,200]{2,1,0:T(8,128)(2,1)}, u32[]{:S(2)}) copy-start(bf16[32,200,200]{2,1,0:T(8,128)(2,1)} %param.6) | copy-start | bytes 7680004
  45.1 427.9 %all-to-all-start.1 = ((bf16[32,6,200,200]{3,2,1,0:T(8,128)(2,1)}), bf16[32,6,200,200]{3,2,1,0:T(8,128)(2,1)}, u32[]{:S(2)}, u32[]{:S(2)}) async-start(bf16[32,6,200,200]{3,2,1,0:T(8,128)(2,1)} %broadcast_select_fusion), calls=%async_computation.1 | async-start | bytes 39321600 | tf_op jit(solution)/shard_map/all_to_all | solution.py:36
  488.3 10.2 %copy-start.2 = (bf16[400,400]{1,0:T(8,128)(2,1)S(1)}, bf16[400,400]{1,0:T(8,128)(2,1)}, u32[]{:S(2)}) copy-start(bf16[400,400]{1,0:T(8,128)(2,1)} %param.9) | copy-start | bytes 960004
  608.9 57.4 %copy-start.1 = (bf16[32,200,200]{2,1,0:T(8,128)(2,1)S(1)}, bf16[32,200,200]{2,1,0:T(8,128)(2,1)}, u32[]{:S(2)}) copy-start(bf16[32,200,200]{2,1,0:T(8,128)(2,1)} %param.6) | copy-start | bytes 7680004
